TPU v7x, 32 devices: a whole 2x2x4 slice. The times are simulated.
32 devices in a mesh: interval: 4 (over x, core), rows: 8 (over z, y).
Axes of the slice: x: 2, y: 2, z: 4, core: 2. Of those that a mesh axis runs over, the one named last changes fastest.
Arguments:
- filtered: float32 [4, 64, 131072], P('interval', None, 'rows'), may hold values from -60 to 60, as said below
- potential: float32 [16, 64, 128], P('rows'), may hold values from 0.5 to 4
Outputs:
- basis: float32 [4, 64, 131072], P('interval', None, 'rows')
- ritz_matrix: float32 [4, 64, 64], P('interval')
- ritz_residual: float32 [4, 64, 131072], P('interval', None, 'rows')
Inputs may be any that keep to these rules, and one draw needn't show every extreme that they name: `filtered`: the rows of each interval's block are linearly independent, and each interval's block shares a part with the block of the interval before it.
All inputs are finite; a program needn't handle non-finite values.
Results may differ from a plain program's by a relative error of at most 0.0003.
Values sent between devices are 32-bit elements; how exact they have to be, the bound alone decides.
A program may use at most 64 MiB of HBM per device.

v0:
```python
import functools

import jax
import jax.numpy as jnp
from jax import lax
from jax.experimental import pallas as pl
from jax.experimental.pallas import tpu as pltpu
from jax.sharding import PartitionSpec as P

MESH = pl.DeviceIdType.MESH
CHUNKS = 8
EARLY = 4
F32 = jnp.float32


def split(x):
    high = x.astype(jnp.bfloat16)
    return high, (x - high.astype(F32)).astype(jnp.bfloat16)


def dot(left, right):
    return jnp.dot(left, right, preferred_element_type=F32)


def dot_nt(left, right):
    return lax.dot_general(left, right, (((1,), (1,)), ((), ())), preferred_element_type=F32)


def product(left, right):
    (lh, ll), (rh, rl) = left, split(right)
    return dot(lh, rh) + (dot(lh, rl) + dot(ll, rh))


def kernel(
    sizes, x_hbm, pot_ref, basis_hbm, ritz_ref, resid_hbm,
    x_ext, p_ext, b_ext, image, sums, gathered, system, weights,
    load_sem, store_sems, own_send, own_recv, halo_send, halo_recv,
    relay_send, relay_recv, sum_send, sum_recv,
):
    parts, intervals, width, plane, line, local = sizes
    tile = plane // CHUNKS
    tiles = local // tile
    own_tile = local // CHUNKS
    me = lax.axis_index("rows")
    interval = lax.axis_index("interval")
    has_before, has_after = me > 0, me < parts - 1
    has_prior, has_next = interval > 0, interval < intervals - 1
    two = 2 * width

    def peer(distance):
        return lax.rem(me + distance, parts)

    barrier = pltpu.get_barrier_semaphore()
    for distance in range(1, parts):
        pl.semaphore_signal(barrier, inc=1, device_id={"rows": peer(distance)}, device_id_type=MESH)

    @pl.when(has_prior)
    def _():
        pl.semaphore_signal(barrier, inc=1, device_id={"interval": interval - 1}, device_id_type=MESH)

    @pl.when(has_next)
    def _():
        pl.semaphore_signal(barrier, inc=1, device_id={"interval": interval + 1}, device_id_type=MESH)

    load = pltpu.make_async_copy(x_hbm, x_ext.at[:, pl.ds(plane, local)], load_sem)
    load.start()
    expected = parts - 1 + jnp.where(has_prior, 1, 0) + jnp.where(has_next, 1, 0)
    pl.semaphore_wait(barrier, expected)

    def own_copy(c):
        return pltpu.make_async_remote_copy(
            x_hbm.at[:, pl.ds(c * own_tile, own_tile)],
            p_ext.at[:, pl.ds(plane + c * own_tile, own_tile)],
            own_send.at[c], own_recv.at[c],
            device_id={"interval": interval + 1}, device_id_type=MESH,
        )

    def halo_copy(side, c):
        start = local - plane if side == 0 else 0
        land = 0 if side == 0 else plane + local
        to = me + 1 if side == 0 else me - 1
        return pltpu.make_async_remote_copy(
            x_hbm.at[:, pl.ds(start + c * tile, tile)],
            x_ext.at[:, pl.ds(land + c * tile, tile)],
            halo_send.at[side, c], halo_recv.at[side, c],
            device_id={"rows": to}, device_id_type=MESH,
        )

    def relay_copy(side, c):
        land = 0 if side == 0 else plane + local
        area = pl.ds(land + c * tile, tile)
        return pltpu.make_async_remote_copy(
            x_ext.at[:, area], p_ext.at[:, area],
            relay_send.at[side, c], relay_recv.at[side, c],
            device_id={"interval": interval + 1}, device_id_type=MESH,
        )

    sends = (has_after, has_before)
    receives = (has_before, has_after)

    def start_halo(c):
        for side in (0, 1):
            @pl.when(sends[side])
            def _():
                halo_copy(side, c).start()

    def relay(c):
        for side in (0, 1):
            @pl.when(receives[side])
            def _():
                halo_copy(side, c).wait_recv()

            @pl.when(receives[side] & has_next)
            def _():
                relay_copy(side, c).start()

    @pl.when(has_next)
    def _():
        for c in range(CHUNKS):
            own_copy(c).start()

    for c in range(EARLY):
        start_halo(c)

    def clear(ref, start, length):
        def step(t, carry):
            at = pl.multiple_of(start + t * tile, 128)
            ref[:, pl.ds(at, tile)] = jnp.zeros((width, tile), F32)
            return carry
        lax.fori_loop(0, length // tile, step, 0)

    for side, land in ((0, 0), (1, plane + local)):
        @pl.when(jnp.logical_not(receives[side]))
        def _():
            clear(x_ext, land, plane)

        @pl.when(jnp.logical_not(receives[side] & has_prior))
        def _():
            clear(p_ext, land, plane)

    @pl.when(jnp.logical_not(has_prior))
    def _():
        clear(p_ext, plane, local)

    load.wait()

    def add_gram(upper, lower):
        high, low = split(jnp.concatenate([upper, lower], axis=0))
        sums[0] += dot_nt(high, high)
        sums[1] += dot_nt(high, low)

    sums[...] = jnp.zeros_like(sums)
    inner_tiles = own_tile // tile
    for c in range(CHUNKS):
        @pl.when(has_prior)
        def _():
            own_copy(c).wait_recv()

        def gram_step(t, carry):
            at = pl.multiple_of(plane + c * own_tile + t * tile, 128)
            add_gram(p_ext[:, pl.ds(at, tile)], x_ext[:, pl.ds(at, tile)])
            return carry
        lax.fori_loop(0, inner_tiles, gram_step, 0)
        if c % 2 == 1 and c // 2 < EARLY:
            relay(c // 2)

    def sum_copy(turn, distance):
        return pltpu.make_async_remote_copy(
            gathered.at[turn, me], gathered.at[turn, me],
            sum_send.at[turn, distance], sum_recv.at[turn, me],
            device_id={"rows": peer(distance)}, device_id_type=MESH,
        )

    def arrival(turn, distance):
        sender = peer(distance)
        return pltpu.make_async_remote_copy(
            gathered.at[turn, sender], gathered.at[turn, sender],
            sum_send.at[turn, distance], sum_recv.at[turn, sender],
            device_id={"rows": sender}, device_id_type=MESH,
        )

    def start_sum(turn):
        gathered[turn, me] = sums[0] + (sums[1] + sums[1].T)
        for distance in range(1, parts):
            sum_copy(turn, distance).start()

    def finish_sum(turn):
        for distance in range(1, parts):
            arrival(turn, distance).wait_recv()
        total = gathered[turn, 0]
        for sender in range(1, parts):
            total = total + gathered[turn, sender]
        return total

    start_sum(0)
    for c in range(EARLY, CHUNKS):
        start_halo(c)
    gram = finish_sum(0)

    rows_at = lax.broadcasted_iota(jnp.int32, (two, two), 0)
    cols_at = lax.broadcasted_iota(jnp.int32, (two, two), 1)
    unit = jnp.where(rows_at == cols_at, 1.0, 0.0).astype(F32)
    lone = jnp.where(interval == 0, 1.0, 0.0).astype(F32)
    system[:, :two] = gram + lone * jnp.where(rows_at < width, unit, 0.0)
    system[:, two:] = unit

    def eliminate(k, carry):
        whole = system[...]
        row = system[pl.ds(k, 1), :]
        lane = lax.broadcasted_iota(jnp.int32, (1, two), 1)
        at = lax.broadcasted_iota(jnp.int32, (two, 1), 0)
        pivot = jnp.sum(jnp.where(lane == k, row[:, :two], 0.0), axis=1, keepdims=True)
        column = jnp.sum(jnp.where(lane == k, whole[:, :two], 0.0), axis=1, keepdims=True)
        scale = lax.rsqrt(pivot)
        scaled = row * scale
        below = jnp.where(at > k, column * scale, 0.0)
        system[...] = jnp.where(at == k, scaled, whole - below * scaled)
        return carry

    relay(EARLY)
    lax.fori_loop(0, width, eliminate, 0)
    relay(EARLY + 1)
    lax.fori_loop(width, two, eliminate, 0)
    for c in range(EARLY + 2, CHUNKS - 1):
        relay(c)
    weights[...] = system[width:, two:]

    def basis_at(at, mixing):
        at = pl.multiple_of(at, 128)
        both = jnp.concatenate([p_ext[:, pl.ds(at, tile)], x_ext[:, pl.ds(at, tile)]], axis=0)
        b_ext[:, pl.ds(at, tile)] = product(mixing, both)

    def own_step(t, carry):
        basis_at(plane + t * tile, split(weights[...]))
        return carry
    lax.fori_loop(0, tiles, own_step, 0)

    basis_out = pltpu.make_async_copy(b_ext.at[:, pl.ds(plane, local)], basis_hbm, store_sems.at[0])
    basis_out.start()

    relay(CHUNKS - 1)
    for c in range(CHUNKS):
        for side in (0, 1):
            @pl.when(receives[side] & has_prior)
            def _():
                relay_copy(side, c).wait_recv()

        for side, land in ((0, 0), (1, plane + local)):
            basis_at(land + c * tile, split(weights[...]))

    sums[...] = jnp.zeros_like(sums)
    lane_at = lax.broadcasted_iota(jnp.int32, (1, tile), 1)
    depth_at = lax.rem(lane_at, line)

    def image_step(t, carry):
        at = t * tile
        here = plane + at
        def near(offset):
            return b_ext[:, pl.ds(pl.multiple_of(here + offset, 128), tile)]
        block = near(0)
        in_plane = lax.rem(at, plane) + lane_at
        beside = near(-plane) + near(plane)
        beside = beside + jnp.where(in_plane >= line, near(-line), 0.0)
        beside = beside + jnp.where(in_plane < plane - line, near(line), 0.0)
        beside = beside + jnp.where(depth_at > 0, pltpu.roll(block, 1, 1), 0.0)
        beside = beside + jnp.where(depth_at < line - 1, pltpu.roll(block, tile - 1, 1), 0.0)
        where = pl.ds(pl.multiple_of(at, 128), tile)
        value = (6.0 + pot_ref[:, where]) * block - beside
        image[:, where] = value
        add_gram(block, value)
        return carry
    lax.fori_loop(0, tiles, image_step, 0)

    start_sum(1)
    projected = finish_sum(1)
    ritz_ref[...] = projected[:width]
    weights[:, :width] = projected[width:, :width]

    def residual_step(t, carry):
        at = pl.multiple_of(t * tile, 128)
        block = b_ext[:, pl.ds(pl.multiple_of(plane + t * tile, 128), tile)]
        image[:, pl.ds(at, tile)] -= product(split(weights[:, :width]), block)
        return carry
    for half in range(2):
        lax.fori_loop(half * (tiles // 2), (half + 1) * (tiles // 2), residual_step, 0)
        area = pl.ds(half * (local // 2), local // 2)
        pltpu.make_async_copy(image.at[:, area], resid_hbm.at[:, area], store_sems.at[1 + half]).start()

    basis_out.wait()
    for half in range(2):
        area = pl.ds(half * (local // 2), local // 2)
        pltpu.make_async_copy(image.at[:, area], resid_hbm.at[:, area], store_sems.at[1 + half]).wait()

    @pl.when(has_next)
    def _():
        for c in range(CHUNKS):
            own_copy(c).wait_send()
    for c in range(CHUNKS):
        for side in (0, 1):
            @pl.when(sends[side])
            def _():
                halo_copy(side, c).wait_send()

            @pl.when(receives[side] & has_next)
            def _():
                relay_copy(side, c).wait_send()
    for turn in (0, 1):
        for distance in range(1, parts):
            sum_copy(turn, distance).wait_send()


def solution(mesh):
    parts, intervals = mesh.shape["rows"], mesh.shape["interval"]

    def body(filtered, potential):
        vectors = filtered[0]
        width, local = vectors.shape
        planes, lines, line = potential.shape
        plane = lines * line
        extended = local + 2 * plane
        sizes = (parts, intervals, width, plane, line, local)
        hbm = pl.BlockSpec(memory_space=pl.ANY)
        vmem = pl.BlockSpec(memory_space=pltpu.VMEM)
        dma = pltpu.SemaphoreType.DMA
        basis, ritz, residual = pl.pallas_call(
            functools.partial(kernel, sizes),
            name="slicing",
            out_shape=(
                jax.ShapeDtypeStruct((width, local), F32),
                jax.ShapeDtypeStruct((width, 2 * width), F32),
                jax.ShapeDtypeStruct((width, local), F32),
            ),
            in_specs=[hbm, vmem],
            out_specs=(hbm, vmem, hbm),
            scratch_shapes=[
                pltpu.VMEM((width, extended), F32),
                pltpu.VMEM((width, extended), F32),
                pltpu.VMEM((width, extended), F32),
                pltpu.VMEM((width, local), F32),
                pltpu.VMEM((2, 2 * width, 2 * width), F32),
                pltpu.VMEM((2, parts, 2 * width, 2 * width), F32),
                pltpu.VMEM((2 * width, 4 * width), F32),
                pltpu.VMEM((width, 2 * width), F32),
                dma, dma((3,)),
                dma((CHUNKS,)), dma((CHUNKS,)),
                dma((2, CHUNKS)), dma((2, CHUNKS)),
                dma((2, CHUNKS)), dma((2, CHUNKS)),
                dma((2, parts)), dma((2, parts)),
            ],
            compiler_params=pltpu.CompilerParams(
                collective_id=0, has_side_effects=True, vmem_limit_bytes=60 * 1024 * 1024
            ),
        )(vectors, potential.reshape(1, local))
        return (basis[None], ritz[None, :, width:], residual[None])

    return jax.shard_map(
        body,
        mesh=mesh,
        in_specs=(P("interval", None, "rows"), P("rows", None, None)),
        out_specs=(
            P("interval", None, "rows"),
            P("interval", None, None),
            P("interval", None, "rows"),
        ),
        check_vma=False,
    )
```

profile of v0, /device:TPU:14, one launch (start us, length us, event | category | flops | bytes accessed | tf_op | source)
XLA Modules:
  0.0 143.3 jit_solution(7377269759965433073)
XLA Ops:
  0.6 134.5 %slicing.1 = (f32[64,16384]{1,0:T(8,128)}, f32[64,128]{1,0:T(8,128)}, f32[64,16384]{1,0:T(8,128)}) custom-call(f32[64,16384]{1,0:T(8,128)} %bitcast.6, f32[1,16384]{1,0:T(1,128)} %bitcast.9), custom_call_target="tpu_custom_call" | custom-call | tf_op jit(solution)/shard_map/slicing/pallas_call | solution.py:325
  135.2 1.4 %slice_bitcast_fusion = f32[1,64,64]{2,1,0:T(8,128)} fusion(f32[64,128]{1,0:T(8,128)} %get-tuple-element.7), kind=kLoop, calls=%fused_computation | loop fusion | bytes 32768 | tf_op jit(solution)/shard_map/broadcast_in_dim | solution.py:354
  136.6 0.0 copy-start
  136.6 4.7 %copy.7 = f32[1,64,16384]{2,1,0:T(8,128)} copy(f32[1,64,16384]{2,1,0:T(8,128)} %bitcast.8) | data formatting | bytes 8388608
  141.3 0.0 copy-done
  141.3 2.0 %copy.8 = f32[1,64,16384]{2,1,0:T(8,128)} copy(f32[1,64,16384]{2,1,0:T(8,128)S(1)} %bitcast.7) | data formatting | bytes 8388608
Async XLA Ops:
  136.6 4.7 %copy-start = (f32[64,16384]{1,0:T(8,128)S(1)}, f32[64,16384]{1,0:T(8,128)}, u32[]{:S(2)}) copy-start(f32[64,16384]{1,0:T(8,128)} %get-tuple-element.8) | copy-start | bytes 12582916
where the time goes:
time: 144 us; the launch traced here: 143 us
  Pallas kernels  135 us (94%)
  local copies, waits for them, and re-layouts  8.12 us (6%)
    pallas_call x1, Pallas kernels, body(): pl.pallas_call(functools.partial(kernel, sizes), name='slicing', out_shap...  135 us
    unnamed x4, local copies, waits for them, and re-layouts  6.67 us

commit v1 on v0

--- a/solution.py
+++ b/solution.py
@@ -9,7 +9,7 @@
 
 MESH = pl.DeviceIdType.MESH
 CHUNKS = 8
-EARLY = 4
+EARLY = 5
 F32 = jnp.float32
 
 
@@ -80,15 +80,15 @@
         land = 0 if side == 0 else plane + local
         to = me + 1 if side == 0 else me - 1
         return pltpu.make_async_remote_copy(
-            x_hbm.at[:, pl.ds(start + c * tile, tile)],
-            x_ext.at[:, pl.ds(land + c * tile, tile)],
+            x_hbm.at[:, pl.ds(pl.multiple_of(start + c * tile, 128), tile)],
+            x_ext.at[:, pl.ds(pl.multiple_of(land + c * tile, 128), tile)],
             halo_send.at[side, c], halo_recv.at[side, c],
             device_id={"rows": to}, device_id_type=MESH,
         )
 
     def relay_copy(side, c):
         land = 0 if side == 0 else plane + local
-        area = pl.ds(land + c * tile, tile)
+        area = pl.ds(pl.multiple_of(land + c * tile, 128), tile)
         return pltpu.make_async_remote_copy(
             x_ext.at[:, area], p_ext.at[:, area],
             relay_send.at[side, c], relay_recv.at[side, c],
@@ -161,8 +161,6 @@
             add_gram(p_ext[:, pl.ds(at, tile)], x_ext[:, pl.ds(at, tile)])
             return carry
         lax.fori_loop(0, inner_tiles, gram_step, 0)
-        if c % 2 == 1 and c // 2 < EARLY:
-            relay(c // 2)
 
     def sum_copy(turn, distance):
         return pltpu.make_async_remote_copy(
@@ -193,8 +191,9 @@
         return total
 
     start_sum(0)
-    for c in range(EARLY, CHUNKS):
-        start_halo(c)
+    start_halo(EARLY)
+    for c in range(EARLY):
+        relay(c)
     gram = finish_sum(0)
 
     rows_at = lax.broadcasted_iota(jnp.int32, (two, two), 0)
@@ -217,12 +216,12 @@
         system[...] = jnp.where(at == k, scaled, whole - below * scaled)
         return carry
 
+    lax.fori_loop(0, width // 2, eliminate, 0)
+    start_halo(EARLY + 1)
+    lax.fori_loop(width // 2, width + width // 2, eliminate, 0)
+    start_halo(EARLY + 2)
     relay(EARLY)
-    lax.fori_loop(0, width, eliminate, 0)
-    relay(EARLY + 1)
-    lax.fori_loop(width, two, eliminate, 0)
-    for c in range(EARLY + 2, CHUNKS - 1):
-        relay(c)
+    lax.fori_loop(width + width // 2, two, eliminate, 0)
     weights[...] = system[width:, two:]
 
     def basis_at(at, mixing):
@@ -238,16 +237,7 @@
     basis_out = pltpu.make_async_copy(b_ext.at[:, pl.ds(plane, local)], basis_hbm, store_sems.at[0])
     basis_out.start()
 
-    relay(CHUNKS - 1)
-    for c in range(CHUNKS):
-        for side in (0, 1):
-            @pl.when(receives[side] & has_prior)
-            def _():
-                relay_copy(side, c).wait_recv()
-
-        for side, land in ((0, 0), (1, plane + local)):
-            basis_at(land + c * tile, split(weights[...]))
-
+    relay(EARLY + 1)
     sums[...] = jnp.zeros_like(sums)
     lane_at = lax.broadcasted_iota(jnp.int32, (1, tile), 1)
     depth_at = lax.rem(lane_at, line)
@@ -269,7 +259,21 @@
         image[:, where] = value
         add_gram(block, value)
         return carry
-    lax.fori_loop(0, tiles, image_step, 0)
+
+    def chunk_step(c, carry):
+        for side, land in ((0, 0), (1, plane + local)):
+            @pl.when(receives[side] & has_prior)
+            def _():
+                relay_copy(side, c).wait_recv()
+            basis_at(land + c * tile, split(weights[...]))
+
+        def plane_step(p, inner):
+            return image_step(p * CHUNKS + c, inner)
+        return lax.fori_loop(0, local // plane, plane_step, carry)
+
+    lax.fori_loop(0, CHUNKS - 1, chunk_step, 0)
+    relay(CHUNKS - 1)
+    chunk_step(CHUNKS - 1, 0)
 
     start_sum(1)
     projected = finish_sum(1)
@@ -348,7 +352,7 @@
                 dma((2, parts)), dma((2, parts)),
             ],
             compiler_params=pltpu.CompilerParams(
-                collective_id=0, has_side_effects=True, vmem_limit_bytes=60 * 1024 * 1024
+                collective_id=0, has_side_effects=True, vmem_limit_bytes=42 * 1024 * 1024
             ),
         )(vectors, potential.reshape(1, local))
         return (basis[None], ritz[None, :, width:], residual[None])

time: 144 us -> 134 us (0.931)
  Pallas kernels: 135 us -> 128 us
  local copies, waits for them, and re-layouts: 8.12 us -> 5.55 us
    pallas_call x1, Pallas kernels: 135 us -> 128 us  [body(): pl.pallas_call(functools.partial(kernel, sizes), name='slicing', out_shap...]
    unnamed x4, local copies, waits for them, and re-layouts: 6.67 us -> 4.86 us
where the time goes in v1:
time: 134 us
  Pallas kernels  128 us (96%)
  local copies, waits for them, and re-layouts  5.55 us (4%)
    pallas_call x1, Pallas kernels, body(): pl.pallas_call(functools.partial(kernel, sizes), name='slicing', out_shap...  128 us
    unnamed x4, local copies, waits for them, and re-layouts  4.86 us

profile of v1, /device:TPU:14, one launch (start us, length us, event | category | flops | bytes accessed | tf_op | source)
XLA Modules:
  0.0 133.8 jit_solution(3685688541517413306)
XLA Ops:
  0.6 0.0 copy-start
  0.6 0.8 copy-done
  1.5 127.6 %slicing.1 = (f32[64,16384]{1,0:T(8,128)S(1)}, f32[64,128]{1,0:T(8,128)S(1)}, f32[64,16384]{1,0:T(8,128)S(1)}) custom-call(f32[64,16384]{1,0:T(8,128)} %bitcast.9, f32[1,16384]{1,0:T(1,128)S(1)} %bitcast.8), custom_call_target="tpu_custom_call" | custom-call | tf_op jit(solution)/shard_map/slicing/pallas_call | solution.py:329
  129.1 0.7 slice_bitcast_fusion
  129.8 2.0 %copy.7 = f32[1,64,16384]{2,1,0:T(8,128)} copy(f32[1,64,16384]{2,1,0:T(8,128)S(1)} %bitcast.7) | data formatting | bytes 8388608
  131.8 2.0 %copy.8 = f32[1,64,16384]{2,1,0:T(8,128)} copy(f32[1,64,16384]{2,1,0:T(8,128)S(1)} %bitcast.6) | data formatting | bytes 8388608
Async XLA Ops:
  0.6 0.8 copy-start

commit v2 on v1

--- a/solution.py
+++ b/solution.py
@@ -9,7 +9,7 @@
 
 MESH = pl.DeviceIdType.MESH
 CHUNKS = 8
-EARLY = 5
+EARLY = 4
 F32 = jnp.float32
 
 
@@ -192,6 +192,7 @@
 
     start_sum(0)
     start_halo(EARLY)
+    start_halo(EARLY + 1)
     for c in range(EARLY):
         relay(c)
     gram = finish_sum(0)
@@ -217,10 +218,9 @@
         return carry
 
     lax.fori_loop(0, width // 2, eliminate, 0)
-    start_halo(EARLY + 1)
+    start_halo(EARLY + 2)
     lax.fori_loop(width // 2, width + width // 2, eliminate, 0)
-    start_halo(EARLY + 2)
-    relay(EARLY)
+    start_halo(EARLY + 3)
     lax.fori_loop(width + width // 2, two, eliminate, 0)
     weights[...] = system[width:, two:]
 
@@ -237,6 +237,7 @@
     basis_out = pltpu.make_async_copy(b_ext.at[:, pl.ds(plane, local)], basis_hbm, store_sems.at[0])
     basis_out.start()
 
+    relay(EARLY)
     relay(EARLY + 1)
     sums[...] = jnp.zeros_like(sums)
     lane_at = lax.broadcasted_iota(jnp.int32, (1, tile), 1)
@@ -271,9 +272,11 @@
             return image_step(p * CHUNKS + c, inner)
         return lax.fori_loop(0, local // plane, plane_step, carry)
 
-    lax.fori_loop(0, CHUNKS - 1, chunk_step, 0)
+    lax.fori_loop(0, EARLY, chunk_step, 0)
+    relay(EARLY + 2)
+    lax.fori_loop(EARLY, EARLY + 2, chunk_step, 0)
     relay(CHUNKS - 1)
-    chunk_step(CHUNKS - 1, 0)
+    lax.fori_loop(EARLY + 2, CHUNKS, chunk_step, 0)
 
     start_sum(1)
     projected = finish_sum(1)

time: 134 us -> 130 us (0.970)
  Pallas kernels: 128 us -> 124 us
    pallas_call x1, Pallas kernels: 128 us -> 124 us  [body(): pl.pallas_call(functools.partial(kernel, sizes), name='slicing', out_shap...]
where the time goes in v2:
time: 130 us
  Pallas kernels  124 us (95%)
  local copies, waits for them, and re-layouts  5.55 us (4%)
    pallas_call x1, Pallas kernels, body(): pl.pallas_call(functools.partial(kernel, sizes), name='slicing', out_shap...  124 us
    unnamed x4, local copies, waits for them, and re-layouts  4.86 us

profile of v2, /device:TPU:14, one launch (start us, length us, event | category | flops | bytes accessed | tf_op | source)
XLA Modules:
  0.0 130.1 jit_solution(6691570353775799724)
XLA Ops:
  0.6 0.0 copy-start
  0.6 0.8 copy-done
  1.5 124.0 %slicing.1 = (f32[64,16384]{1,0:T(8,128)S(1)}, f32[64,128]{1,0:T(8,128)S(1)}, f32[64,16384]{1,0:T(8,128)S(1)}) custom-call(f32[64,16384]{1,0:T(8,128)} %bitcast.9, f32[1,16384]{1,0:T(1,128)S(1)} %bitcast.8), custom_call_target="tpu_custom_call" | custom-call | tf_op jit(solution)/shard_map/slicing/pallas_call | solution.py:332
  125.4 0.7 slice_bitcast_fusion
  126.1 2.0 %copy.7 = f32[1,64,16384]{2,1,0:T(8,128)} copy(f32[1,64,16384]{2,1,0:T(8,128)S(1)} %bitcast.7) | data formatting | bytes 8388608
  128.1 2.0 %copy.8 = f32[1,64,16384]{2,1,0:T(8,128)} copy(f32[1,64,16384]{2,1,0:T(8,128)S(1)} %bitcast.6) | data formatting | bytes 8388608
Async XLA Ops:
  0.6 0.8 copy-start

commit v3 on v2

--- a/solution.py
+++ b/solution.py
@@ -237,8 +237,6 @@
     basis_out = pltpu.make_async_copy(b_ext.at[:, pl.ds(plane, local)], basis_hbm, store_sems.at[0])
     basis_out.start()
 
-    relay(EARLY)
-    relay(EARLY + 1)
     sums[...] = jnp.zeros_like(sums)
     lane_at = lax.broadcasted_iota(jnp.int32, (1, tile), 1)
     depth_at = lax.rem(lane_at, line)
@@ -273,7 +271,8 @@
         return lax.fori_loop(0, local // plane, plane_step, carry)
 
     lax.fori_loop(0, EARLY, chunk_step, 0)
-    relay(EARLY + 2)
+    for c in range(EARLY, CHUNKS - 1):
+        relay(c)
     lax.fori_loop(EARLY, EARLY + 2, chunk_step, 0)
     relay(CHUNKS - 1)
     lax.fori_loop(EARLY + 2, CHUNKS, chunk_step, 0)

time: 130 us -> 136 us (1.046)
  Pallas kernels: 124 us -> 130 us
    pallas_call x1, Pallas kernels: 124 us -> 130 us  [body(): pl.pallas_call(functools.partial(kernel, sizes), name='slicing', out_shap...]
where the time goes in v3:
time: 136 us
  Pallas kernels  130 us (96%)
  local copies, waits for them, and re-layouts  5.55 us (4%)
    pallas_call x1, Pallas kernels, body(): pl.pallas_call(functools.partial(kernel, sizes), name='slicing', out_shap...  130 us
    unnamed x4, local copies, waits for them, and re-layouts  4.86 us

profile of v3, /device:TPU:14, one launch (start us, length us, event | category | flops | bytes accessed | tf_op | source)
XLA Modules:
  0.0 136.3 jit_solution(5648564006231796016)
XLA Ops:
  0.6 0.0 copy-start
  0.6 0.8 copy-done
  1.5 130.1 %slicing.1 = (f32[64,16384]{1,0:T(8,128)S(1)}, f32[64,128]{1,0:T(8,128)S(1)}, f32[64,16384]{1,0:T(8,128)S(1)}) custom-call(f32[64,16384]{1,0:T(8,128)} %bitcast.9, f32[1,16384]{1,0:T(1,128)S(1)} %bitcast.8), custom_call_target="tpu_custom_call" | custom-call | tf_op jit(solution)/shard_map/slicing/pallas_call | solution.py:331
  131.5 0.7 slice_bitcast_fusion
  132.2 2.0 %copy.7 = f32[1,64,16384]{2,1,0:T(8,128)} copy(f32[1,64,16384]{2,1,0:T(8,128)S(1)} %bitcast.7) | data formatting | bytes 8388608
  134.2 2.0 %copy.8 = f32[1,64,16384]{2,1,0:T(8,128)} copy(f32[1,64,16384]{2,1,0:T(8,128)S(1)} %bitcast.6) | data formatting | bytes 8388608
Async XLA Ops:
  0.6 0.8 copy-start
